TPU v7x, 32 devices: a whole 2x2x4 slice. The times are simulated.
32 devices in a mesh: ep: 2 (over core), fsdp: 16 (over z, y, x).
Axes of the slice: x: 2, y: 2, z: 4, core: 2. Of those that a mesh axis runs over, the one named last changes fastest.
Arguments:
- train_down: float32 [8, 14336, 4096], P('ep', None, 'fsdp'), may hold values from -0.0625 to 0.0625
- router_weight: float32 [4096, 8], P('fsdp', 'ep'), may hold values from -0.09375 to 0.09375
- router_gain: float32 [4096], P('fsdp'), may hold values from 0.25 to 1.75
Outputs:
- ready_down: bfloat16 [8, 14336, 4096], P('ep', 'fsdp')
- scale_down: float32 [8, 14336], P('ep', 'fsdp')
- serve_router: bfloat16 [4096, 8], replicated
All inputs are finite; a program needn't handle non-finite values.
Results may differ from a plain program's by a relative error of at most 0.001.
Values may be sent and summed in bfloat16 or wider, within the bound.
A program may use at most 192 MiB of HBM per device.

v0:
```python
import jax
import jax.numpy as jnp
from jax import lax
from jax.sharding import PartitionSpec as P


def body(train_down, router_weight, router_gain):
    total_down = lax.psum(jnp.sum(train_down * train_down, axis=2), "fsdp")
    scale_down = jnp.sqrt(total_down)
    narrow_down = (train_down / jnp.expand_dims(scale_down, 2)).astype(jnp.bfloat16)
    ready_down = lax.all_to_all(narrow_down, "fsdp", split_axis=1, concat_axis=2, tiled=True)
    scale_down = lax.dynamic_slice_in_dim(
        scale_down, lax.axis_index("fsdp") * ready_down.shape[1], ready_down.shape[1], axis=1
    )
    part_router = (router_weight * router_gain[:, None]).astype(jnp.bfloat16)
    row_router = lax.all_gather(part_router, "fsdp", axis=0, tiled=True)
    serve_router = lax.all_gather(row_router, "ep", axis=1, tiled=True)
    return (ready_down, scale_down, serve_router)


def solution(mesh):
    placed = (P("ep", None, "fsdp"), P("fsdp", "ep"), P("fsdp"))
    return jax.shard_map(
        body,
        mesh=mesh,
        in_specs=placed,
        out_specs=(P("ep", "fsdp", None), P("ep", "fsdp"), P()),
        check_vma=False,
    )
```

profile of v0, /device:TPU:11, one launch (start us, length us, event | category | flops | bytes accessed | tf_op | source)
XLA Modules:
  0.0 972.7 jit_solution(4918430820290216060)
XLA Ops:
  7.2 0.0 all-reduce.2.cloned.1.call-start
  7.2 19.4 %multiply_reduce_fusion = f32[4,14336]{1,0:T(4,128)} fusion(f32[4,14336,256]{2,1,0:T(8,128)} %param.3), kind=kLoop, calls=%fused_computation.1 | loop fusion | flops 29302784 | bytes 58949632 | tf_op jit(solution)/shard_map/reduce_sum | solution.py:8
  26.6 0.0 all-reduce.2.cloned.1.call-update
  26.7 106.3 %all-reduce.2.cloned.1.call-done = f32[4,14336]{1,0:T(4,128)} async-done(((f32[4,14336]{1,0:T(4,128)}), f32[4,14336]{1,0:T(4,128)}) %all-reduce.2.cloned.1.call-update) | async-done | bytes 229392 | tf_op jit(solution)/shard_map/psum | solution.py:8
  132.9 1.0 sqrt.3
  134.0 4.7 copy.7
  138.6 0.0 copy-start
  138.6 0.0 copy-start.1
  138.6 65.1 %fusion = bf16[4,14336,256]{2,0,1:T(4,128)(2,1)} fusion(f32[4,14336,256]{2,1,0:T(8,128)} %param.3, f32[4,14336]{0,1:T(8,128)} %copy.7), kind=kLoop, calls=%fused_computation.2 | loop fusion | flops 29360128 | bytes 88309760 | tf_op jit(solution)/shard_map/convert_element_type | solution.py:10
  203.8 6.1 all-to-all-start
  209.9 0.0 copy-done
  209.9 0.0 copy-done.1
  209.9 672.0 %all_gather.6 = bf16[4096,4]{0,1:T(4,128)(2,1)S(1)} all-gather(bf16[256,4]{0,1:T(4,128)(2,1)S(1)} %multiply_convert_fusion), channel_id=1, replica_groups=mesh['ep'=2,'fsdp'=16] {'fsdp'}, dimensions={0}, use_global_device_ids=true | all-gather | bytes 34816 | tf_op jit(solution)/shard_map/all_gather | solution.py:16
  881.9 11.4 %all-gather = bf16[2,4,4096]{2,1,0:T(4,128)(2,1)S(1)} all-gather(bf16[1,4,4096]{2,1,0:T(4,128)(2,1)S(1)} %bitcast.9), channel_id=1, replica_groups=mesh['ep'=2,'fsdp'=16] {'ep'}, dimensions={0}, use_global_device_ids=true | all-gather | bytes 98304 | tf_op jit(solution)/shard_map/all_gather | solution.py:17
  893.3 0.7 reshape.9
  894.0 0.6 constant_dynamic-slice_fusion
  894.6 0.0 all-to-all-done
  894.6 27.5 %copy.9 = bf16[4,896,16,256]{3,2,1,0:T(8,128)(2,1)} copy(bf16[4,896,16,256]{3,0,1,2:T(4,128)(2,1)} %bitcast.1) | data formatting | bytes 58720256 | tf_op jit(solution)/shard_map/all_to_all | solution.py:11
  922.1 43.7 %all_to_all.16 = bf16[4,896,4096]{2,1,0:T(8,128)(2,1)} reshape(bf16[4,896,16,256]{3,2,1,0:T(8,128)(2,1)} %copy.9) | data formatting | bytes 58720256 | tf_op jit(solution)/shard_map/all_to_all | solution.py:11
  (1 shorter events, 0.0 us)
Async XLA Ops:
  7.2 125.8 %all-reduce.2.cloned.1.call-start = ((), (), s32[]{:S(2)}) async-start(), calls=%async_computation.1 | async-start | bytes 458752 | tf_op jit(solution)/shard_map/psum | solution.py:8
  138.6 71.3 %copy-start = (f32[256,4]{0,1:T(4,128)S(1)}, f32[256,4]{0,1:T(4,128)}, u32[]{:S(2)}) copy-start(f32[256,4]{0,1:T(4,128)} %param.4) | copy-start | bytes 12292
  138.6 71.3 %copy-start.1 = (f32[256]{0:T(256)S(1)}, f32[256]{0:T(256)}, u32[]{:S(2)}) copy-start(f32[256]{0:T(256)} %param.5) | copy-start | bytes 3076
  203.8 690.8 %all-to-all-start = ((bf16[4,14336,256]{2,0,1:T(4,128)(2,1)}), bf16[4,14336,256]{2,0,1:T(4,128)(2,1)}, u32[]{:S(2)}, u32[]{:S(2)}) async-start(bf16[4,14336,256]{2,0,1:T(4,128)(2,1)} %fusion), calls=%async_computation | async-start | bytes 58720256 | tf_op jit(solution)/shard_map/all_to_all | solution.py:11
Sparse Core Ops, SparseCore 0:
  26.8 106.1 all-reduce.1
where the time goes:
time: 974 us; the launch traced here: 973 us
  blocking collectives  683 us (70%)
  waiting for transfers between devices  106 us (11%)
  other arithmetic  84.6 us (9%)
  local copies, waits for them, and re-layouts  78.2 us (8%)
  between operations  14.1 us (1%)
    all_gather x1, blocking collectives, body(): row_router = lax.all_gather(part_router, 'fsdp', axis=0, tiled=True)  672 us
    psum x1, waiting for transfers between devices, body(): total_down = lax.psum(jnp.sum(train_down * train_down, axis=2), 'fsdp')  106 us
    all_to_all x2, local copies, waits for them, and re-layouts, body(): lax.all_to_all(narrow_down, 'fsdp', split_axis=1, concat_axis=2, tiled=True)  71.2 us
    convert_element_type x1, other arithmetic, body(): (train_down / jnp.expand_dims(scale_down, 2)).astype(jnp.bfloat16)  65.1 us
  transfers between devices with their start and end apart: 2, of which 1 were waited for; matrix products, arithmetic and copies ran while one was open for 0% of the time, Pallas kernels for 0%

commit v1 on v0

--- a/solution.py
+++ b/solution.py
@@ -5,7 +5,8 @@
 
 
 def body(train_down, router_weight, router_gain):
-    total_down = lax.psum(jnp.sum(train_down * train_down, axis=2), "fsdp")
+    sheet = jnp.sum(train_down * train_down, axis=2)
+    total_down = jnp.sum(lax.all_gather(sheet, axis_name="fsdp"), 0)
     scale_down = jnp.sqrt(total_down)
     narrow_down = (train_down / jnp.expand_dims(scale_down, 2)).astype(jnp.bfloat16)
     ready_down = lax.all_to_all(narrow_down, "fsdp", split_axis=1, concat_axis=2, tiled=True)

time: 974 us -> 941 us (0.966)
  waiting for transfers between devices: 106 us -> 71.6 us
    psum x1 -> x0, waiting for transfers between devices: 106 us -> none  [body(): total_down = lax.psum(jnp.sum(train_down * train_down, axis=2), 'fsdp')]
    all_gather x0 -> x1, waiting for transfers between devices: none -> 71.6 us  [body(): total_down = jnp.sum(lax.all_gather(sheet, axis_name='fsdp'), 0)]
    reduce_sum x1 -> x2, other arithmetic: 19.4 us -> 22.1 us  [the longest x1 19.4 us: body(): sheet = jnp.sum(train_down * train_down, axis=2)]
where the time goes in v1:
time: 941 us; the launch traced here: 939 us
  blocking collectives  684 us (73%)
  other arithmetic  87.2 us (9%)
  local copies, waits for them, and re-layouts  77.3 us (8%)
  waiting for transfers between devices  71.6 us (8%)
  between operations  14.1 us (1%)
    all_gather x1, blocking collectives, body(): row_router = lax.all_gather(part_router, 'fsdp', axis=0, tiled=True)  672 us
    all_gather x1, waiting for transfers between devices, body(): total_down = jnp.sum(lax.all_gather(sheet, axis_name='fsdp'), 0)  71.6 us
    all_to_all x2, local copies, waits for them, and re-layouts, body(): lax.all_to_all(narrow_down, 'fsdp', split_axis=1, concat_axis=2, tiled=True)  71.2 us
    convert_element_type x1, other arithmetic, body(): (train_down / jnp.expand_dims(scale_down, 2)).astype(jnp.bfloat16)  65.1 us
    reduce_sum x1, other arithmetic, body(): sheet = jnp.sum(train_down * train_down, axis=2)  19.4 us
  transfers between devices with their start and end apart: 2, of which 1 were waited for; matrix products, arithmetic and copies ran while one was open for 0% of the time, Pallas kernels for 0%

profile of v1, /device:TPU:11, one launch (start us, length us, event | category | flops | bytes accessed | tf_op | source)
XLA Modules:
  0.0 939.5 jit_solution(7723646013048486692)
XLA Ops:
  7.2 0.0 all-gather.5.cloned.1.call-start
  7.2 19.4 %multiply_reduce_fusion = f32[4,14336]{1,0:T(4,128)} fusion(f32[4,14336,256]{2,1,0:T(8,128)} %param.3), kind=kLoop, calls=%fused_computation.1 | loop fusion | flops 29302784 | bytes 58949632 | tf_op jit(solution)/shard_map/reduce_sum | solution.py:8
  26.6 0.0 all-gather.5.cloned.1.call-update
  26.7 71.6 %all-gather.5.cloned.1.call-done = f32[16,4,14336]{2,1,0:T(4,128)} async-done(((f32[1,4,14336]{2,1,0:T(4,128)}), f32[16,4,14336]{2,1,0:T(4,128)}) %all-gather.5.cloned.1.call-update) | async-done | bytes 3670032 | tf_op jit(solution)/shard_map/all_gather | solution.py:9
  98.3 2.6 reduce_sum.19
  100.9 0.1 sqrt.7
  101.0 4.7 copy.7
  105.7 65.1 %fusion = bf16[4,14336,256]{2,0,1:T(4,128)(2,1)} fusion(f32[4,14336,256]{2,1,0:T(8,128)} %param.3, f32[4,14336]{0,1:T(8,128)} %copy.7), kind=kLoop, calls=%fused_computation.2 | loop fusion | flops 29360128 | bytes 88309760 | tf_op jit(solution)/shard_map/convert_element_type | solution.py:11
  170.8 0.0 copy-start
  170.8 0.0 copy-start.1
  170.8 5.7 all-to-all-start
  176.5 0.0 copy-done
  176.5 0.0 copy-done.1
  176.5 672.2 %all_gather.14 = bf16[4096,4]{0,1:T(4,128)(2,1)S(1)} all-gather(bf16[256,4]{0,1:T(4,128)(2,1)S(1)} %multiply_convert_fusion), channel_id=1, replica_groups=mesh['ep'=2,'fsdp'=16] {'fsdp'}, dimensions={0}, use_global_device_ids=true | all-gather | bytes 34816 | tf_op jit(solution)/shard_map/all_gather | solution.py:17
  848.7 11.4 %all-gather.2 = bf16[2,4,4096]{2,1,0:T(4,128)(2,1)S(1)} all-gather(bf16[1,4,4096]{2,1,0:T(4,128)(2,1)S(1)} %bitcast.11), channel_id=1, replica_groups=mesh['ep'=2,'fsdp'=16] {'ep'}, dimensions={0}, use_global_device_ids=true | all-gather | bytes 98304 | tf_op jit(solution)/shard_map/all_gather | solution.py:18
  860.1 0.7 reshape.14
  860.8 0.6 constant_dynamic-slice_fusion
  861.4 0.0 all-to-all-done
  861.4 27.5 %copy.9 = bf16[4,896,16,256]{3,2,1,0:T(8,128)(2,1)} copy(bf16[4,896,16,256]{3,0,1,2:T(4,128)(2,1)} %bitcast.2) | data formatting | bytes 58720256 | tf_op jit(solution)/shard_map/all_to_all | solution.py:12
  888.9 43.7 %all_to_all.16 = bf16[4,896,4096]{2,1,0:T(8,128)(2,1)} reshape(bf16[4,896,16,256]{3,2,1,0:T(8,128)(2,1)} %copy.9) | data formatting | bytes 58720256 | tf_op jit(solution)/shard_map/all_to_all | solution.py:12
  (1 shorter events, 0.0 us)
Async XLA Ops:
  7.2 91.1 %all-gather.5.cloned.1.call-start = ((), (), s32[]{:S(2)}) async-start(), calls=%async_computation.1 | async-start | bytes 3899392 | tf_op jit(solution)/shard_map/all_gather | solution.py:9
  170.8 5.7 copy-start
  170.8 5.7 copy-start.1
  170.8 690.5 %all-to-all-start = ((bf16[4,14336,256]{2,0,1:T(4,128)(2,1)}), bf16[4,14336,256]{2,0,1:T(4,128)(2,1)}, u32[]{:S(2)}, u32[]{:S(2)}) async-start(bf16[4,14336,256]{2,0,1:T(4,128)(2,1)} %fusion), calls=%async_computation | async-start | bytes 58720256 | tf_op jit(solution)/shard_map/all_to_all | solution.py:12
Sparse Core Ops, SparseCore 0:
  26.8 71.4 all-gather.4
